TPU v7x, 32 devices: a whole 2x2x4 slice. The times are simulated.
32 devices in a mesh: ens: 2 (over core), ctx: 4 (over y, x), group: 4 (over z).
Axes of the slice: x: 2, y: 2, z: 4, core: 2. Of those that a mesh axis runs over, the one named last changes fastest.
Arguments:
- latents: bfloat16 [8, 1024, 512], P('ens', ('ctx', 'group')), parts along dimension 0, may hold values from -6 to 6
- rotary_rows: bfloat16 [8, 1024, 64], P('ens', ('ctx', 'group')), parts along dimension 0, may hold values from -6 to 6
- latent_gain: float32 [512], replicated, may hold values from 0.25 to 1.75
- key_up: bfloat16 [1024, 16, 128], P('ens', 'group'), parts along dimension 0, may hold values from -0.25 to 0.25
- value_up: bfloat16 [1024, 16, 128], P('ens', 'group'), parts along dimension 0, may hold values from -0.25 to 0.25
Outputs:
- stored_keys: bfloat16 [8, 16, 192, 1024], P(('ens', 'ctx'), 'group'), parts along dimension 0
- stored_values: bfloat16 [8, 1024, 16, 128], P(('ens', 'ctx'), None, 'group'), parts along dimension 0
There are 2 independent parts, one for each index of `ens`. A program takes and returns all parts, laid end to end along the dimension named above; an argument that names none is the same for every part. Nothing has to cross between parts.
All inputs are finite; a program needn't handle non-finite values.
Results may differ from a plain program's by a relative error of at most 0.0049.
Values may be sent and summed in bfloat16 or wider, within the bound.
A program may use at most 64 MiB of HBM per device.

v0:
```python
import jax
import jax.numpy as jnp
from jax import lax
from jax.sharding import PartitionSpec as P


def to_heads(rows, rotary, key_up, value_up):
    wide_keys = jnp.einsum(
        "btr,rhk->bthk", rows, key_up, preferred_element_type=jnp.float32
    ).astype(jnp.bfloat16)
    shared = jnp.broadcast_to(rotary[:, :, None], wide_keys.shape[:3] + rotary.shape[2:])
    wide_values = jnp.einsum(
        "btr,rhk->bthk", rows, value_up, preferred_element_type=jnp.float32
    ).astype(jnp.bfloat16)
    return (jnp.concatenate([wide_keys, shared], axis=-1), wide_values)


def root_norm(vectors, row_gain):
    return (
        vectors * lax.rsqrt(jnp.mean(vectors * vectors, axis=-1, keepdims=True) + 1e-06) * row_gain
    )


def per_device(latents, rotary_rows, latent_gain, key_up, value_up):
    rows_ready = root_norm(latents.astype(jnp.float32), latent_gain).astype(jnp.bfloat16)
    rows_moved, rotary_moved = (
        lax.all_to_all(rows_ready, "ctx", split_axis=0, concat_axis=1, tiled=True),
        lax.all_to_all(rotary_rows, "ctx", split_axis=0, concat_axis=1, tiled=True),
    )
    rows_cut = rows_moved.reshape(
        rows_moved.shape[0], lax.axis_size("ctx"), -1, rows_moved.shape[2]
    )
    rotary_cut = rotary_moved.reshape(
        rotary_moved.shape[0], lax.axis_size("ctx"), -1, rotary_moved.shape[2]
    )
    rows_joined, rotary_joined = (
        lax.all_gather(rows_cut, "group", axis=2, tiled=True),
        lax.all_gather(rotary_cut, "group", axis=2, tiled=True),
    )
    rows_whole = rows_joined.reshape(rows_joined.shape[0], -1, rows_joined.shape[3])
    rotary_whole = rotary_joined.reshape(rotary_joined.shape[0], -1, rotary_joined.shape[3])
    stored_keys, stored_values = to_heads(rows_whole, rotary_whole, key_up, value_up)
    stored_keys = jnp.transpose(stored_keys, (0, 2, 3, 1))
    return (stored_keys, stored_values)


def solution(mesh):
    in_specs = (
        P("ens", ("ctx", "group"), None),
        P("ens", ("ctx", "group"), None),
        P(),
        P("ens", "group", None),
        P("ens", "group", None),
    )
    out_specs = (P(("ens", "ctx"), "group", None, None), P(("ens", "ctx"), None, "group", None))
    return jax.shard_map(
        per_device, mesh=mesh, in_specs=in_specs, out_specs=out_specs, check_vma=False
    )
```

profile of v0, /device:TPU:0, one launch (start us, length us, event | category | flops | bytes accessed | tf_op | source)
XLA Modules:
  0.0 66.3 jit_solution(5958426524506298335)
XLA Ops:
  7.2 0.0 copy-start
  7.2 0.0 copy-start.2
  7.2 0.0 all-gather.4.cloned.1.call-start
  7.2 1.2 %fusion.1 = f32[4,64]{1,0:T(4,128)S(1)} fusion(bf16[4,64,512]{2,1,0:T(8,128)(2,1)} %param.5), kind=kLoop, calls=%fused_computation.6 | loop fusion | flops 392960 | bytes 263168 | tf_op jit(solution)/shard_map/reduce_sum | solution.py:20
  8.4 1.1 %fusion.3 = bf16[4,64,512]{2,1,0:T(8,128)(2,1)S(1)} fusion(bf16[4,64,512]{2,1,0:T(8,128)(2,1)} %param.5, f32[512]{0:T(512)} %param.7, f32[4,64]{1,0:T(4,128)S(1)} %add_rsqrt_fusion), kind=kLoop, calls=%fused_computation.8 | loop fusion | flops 524288 | bytes 527360 | tf_op jit(solution)/shard_map/convert_element_type | solution.py:25
  9.5 10.8 %all_to_all.8 = bf16[4,64,512]{2,1,0:T(8,128)(2,1)} all-to-all(bf16[4,64,512]{2,1,0:T(8,128)(2,1)S(1)} %fusion.3), channel_id=1, replica_groups=mesh['ens'=2,'ctx'=4,'group'=4] {'ctx'}, dimensions={0} | all-to-all | bytes 524288 | tf_op jit(solution)/shard_map/all_to_all | solution.py:27
  20.3 0.0 all-gather.4.cloned.1.call-update
  20.4 1.6 %reshape.51 = bf16[4,2,2048]{2,1,0:T(2,128)(2,1)} reshape(bf16[4,64,64]{2,1,0:T(8,128)(2,1)} %param.6) | data formatting | bytes 65536
  21.9 3.3 %all-to-all-start.1 = ((bf16[4,2,2048]{2,1,0:T(2,128)(2,1)}), bf16[4,2,2048]{2,1,0:T(2,128)(2,1)S(1)}, u32[]{:S(2)}, u32[]{:S(2)}) async-start(bf16[4,2,2048]{2,1,0:T(2,128)(2,1)} %reshape.51), calls=%async_computation.1 | async-start | bytes 65536 | tf_op jit(solution)/shard_map/all_to_all | solution.py:28
  25.2 0.0 copy-done.2
  25.2 0.3 copy.7
  25.5 4.4 %all-to-all-done.1 = bf16[4,2,2048]{2,1,0:T(2,128)(2,1)S(1)} async-done(((bf16[4,2,2048]{2,1,0:T(2,128)(2,1)}), bf16[4,2,2048]{2,1,0:T(2,128)(2,1)S(1)}, u32[]{:S(2)}, u32[]{:S(2)}) %all-to-all-start.1) | async-done | bytes 32800 | tf_op jit(solution)/shard_map/all_to_all | solution.py:28
  29.9 0.1 reshape.52
  30.0 16.7 %all-gather.1 = bf16[4,256,64]{2,1,0:T(8,128)(2,1)S(1)} all-gather(bf16[4,64,64]{2,1,0:T(8,128)(2,1)S(1)} %reshape.52), channel_id=3, replica_groups=mesh['ens'=2,'ctx'=4,'group'=4] {'group'}, dimensions={1}, use_global_device_ids=true | all-gather | bytes 163840 | tf_op jit(solution)/shard_map/all_gather | solution.py:38
  46.8 0.1 copy.8
  46.9 5.5 %all-gather.4.cloned.1.call-done = bf16[4,256,512]{2,1,0:T(8,128)(2,1)} async-done(((bf16[4,64,512]{2,1,0:T(8,128)(2,1)}), bf16[4,256,512]{2,1,0:T(8,128)(2,1)}) %all-gather.4.cloned.1.call-update) | async-done | bytes 1048592 | tf_op jit(solution)/shard_map/all_gather | solution.py:37
  52.4 2.0 %fusion.5 = f32[1024,512]{0,1:S(1)} fusion(bf16[1024,512]{1,0:T(8,128)(2,1)} %bitcast.17, bf16[512,512]{0,1:T(8,128)(2,1)S(1)} %bitcast.16), kind=kOutput, calls=%fused_computation.11 | convolution fusion | flops 536870912 | bytes 3670016
  54.4 0.0 copy-start.1
  54.4 0.2 convert_bitcast_fusion
  54.6 0.0 copy-done
  54.6 1.0 %copy-done.1 = bf16[4,256,512]{2,1,0:T(8,128)(2,1)S(1)} copy-done((bf16[4,256,512]{2,1,0:T(8,128)(2,1)S(1)}, bf16[4,256,512]{2,1,0:T(8,128)(2,1)}, u32[]{:S(2)}) %copy-start.1) | copy-done | bytes 1048600
  55.6 0.7 %fusion = bf16[1,1024,4,128]{3,1,2,0:T(8,128)(2,1)S(1)} fusion(bf16[1024,512,1]{1,0,2:T(8,128)(2,1)S(1)} %bitcast.18, bf16[512,4,128]{2,1,0:T(4,128)(2,1)S(1)} %copy-done), kind=kOutput, calls=%fused_computation.2 | convolution fusion | flops 537395200 | bytes 2621440 | tf_op jit(solution)/shard_map/btr,rhk->bthk/dot_general | solution.py:12
  56.3 1.8 %copy.10 = bf16[1,1024,4,128]{3,2,1,0:T(4,128)(2,1)} copy(bf16[1,1024,4,128]{3,1,2,0:T(8,128)(2,1)S(1)} %fusion) | data formatting | bytes 2097152
  58.1 0.1 broadcast_in_dim.10
  58.2 1.3 %maximum_bitcast_fusion = bf16[1,4,192,1024]{3,2,1,0:T(8,128)(2,1)} fusion(bf16[1,1024,4,64]{1,3,2,0:T(8,128)(2,1)S(1)} %broadcast_in_dim.10, bf16[1,1024,4,128]{1,3,2,0:T(8,128)(2,1)S(1)} %convert_bitcast_fusion), kind=kLoop, calls=%fused_computation | loop fusion | flops 3145728 | bytes 3145728 | tf_op jit(solution)/shard_map/transpose | solution.py:43
  (1 shorter events, 0.0 us)
Async XLA Ops:
  7.2 47.4 %copy-start = (bf16[512,4,128]{2,1,0:T(4,128)(2,1)S(1)}, bf16[512,4,128]{2,1,0:T(4,128)(2,1)}, u32[]{:S(2)}) copy-start(bf16[512,4,128]{2,1,0:T(4,128)(2,1)} %param.9) | copy-start | bytes 1572868
  7.2 18.0 %copy-start.2 = (bf16[512,4,128]{2,1,0:T(4,128)(2,1)S(1)}, bf16[512,4,128]{2,1,0:T(4,128)(2,1)}, u32[]{:S(2)}) copy-start(bf16[512,4,128]{2,1,0:T(4,128)(2,1)} %param.8) | copy-start | bytes 1572868
  7.2 45.2 %all-gather.4.cloned.1.call-start = ((), (), s32[]{:S(2)}) async-start(), calls=%async_computation.2 | async-start | bytes 1310720 | tf_op jit(solution)/shard_map/all_gather | solution.py:37
  21.9 8.0 %all-to-all-start.1 = ((bf16[4,2,2048]{2,1,0:T(2,128)(2,1)}), bf16[4,2,2048]{2,1,0:T(2,128)(2,1)S(1)}, u32[]{:S(2)}, u32[]{:S(2)}) async-start(bf16[4,2,2048]{2,1,0:T(2,128)(2,1)} %reshape.51), calls=%async_computation.1 | async-start | bytes 65536 | tf_op jit(solution)/shard_map/all_to_all | solution.py:28
  54.4 1.2 %copy-start.1 = (bf16[4,256,512]{2,1,0:T(8,128)(2,1)S(1)}, bf16[4,256,512]{2,1,0:T(8,128)(2,1)}, u32[]{:S(2)}) copy-start(bf16[4,256,512]{2,1,0:T(8,128)(2,1)} %all-gather.4.cloned.1.call-done) | copy-start | bytes 3145732
Sparse Core Ops, SparseCore 0:
  20.5 31.8 all-gather.3
where the time goes:
time: 66.7 us; the launch traced here: 66.3 us
  blocking collectives  27.5 us (41%)
  between operations  14.1 us (21%)
  waiting for transfers between devices  9.92 us (15%)
  local copies, waits for them, and re-layouts  5.03 us (8%)
  other arithmetic  3.68 us (6%)
  starting transfers between devices  3.3 us (5%)
  matrix products  2.67 us (4%)
    all_gather x1, blocking collectives, per_device(): lax.all_gather(rotary_cut, 'group', axis=2, tiled=True)  16.7 us
    all_to_all x1, blocking collectives, per_device(): lax.all_to_all(rows_ready, 'ctx', split_axis=0, concat_axis=1, tiled=True)  10.8 us
    all_gather x1, waiting for transfers between devices, per_device(): lax.all_gather(rows_cut, 'group', axis=2, tiled=True)  5.51 us
    unnamed x10, local copies, waits for them, and re-layouts  4.85 us
    all_to_all x1, waiting for transfers between devices, per_device(): lax.all_to_all(rotary_rows, 'ctx', split_axis=0, concat_axis=1, tiled=True)  4.39 us
    all_to_all x1, starting transfers between devices, per_device(): lax.all_to_all(rotary_rows, 'ctx', split_axis=0, concat_axis=1, tiled=True)  3.26 us
    unnamed x1, matrix products  1.96 us
  transfers between devices with their start and end apart: 2, of which 2 were waited for; matrix products, arithmetic and copies ran while one was open for 3% of the time, Pallas kernels for 0%

commit v1 on v0

v1 whole, which is shorter than its diff:
```python
import functools

import jax
import jax.numpy as jnp
from jax import lax
from jax.experimental import pallas as pl
from jax.experimental.pallas import tpu as pltpu
from jax.sharding import PartitionSpec as P

MESH = pl.DeviceIdType.MESH
UNIT = 128


def partner(me, step, count):
    if count & (count - 1):
        return lax.rem(me + step, count)
    total, bit = 0, 1
    while bit < count:
        total = total + bit * lax.rem(me // bit + step // bit, 2)
        bit *= 2
    return total


def kernel(
    seqs, planes, heads,
    lat, rot, gain_in, key_up, value_up, keys, values,
    stage, raw, rot_stage, rot_pack, rot_raw, key_stage, value_stage,
    wide, key_w, value_w, mixed, gain,
    local_sem, got, got_rot, up, up_rot, down, down_rot, side, side_rot,
):
    c, g = lax.axis_index("ctx"), lax.axis_index("group")
    blk, latent = raw.shape[2], raw.shape[3]
    rotary = rot_stage.shape[2]
    half = blk // 2
    per_unit = UNIT // blk
    key_part = key_w.shape[0] // heads

    loads = [
        pltpu.make_async_copy(lat, stage, local_sem.at[0]),
        pltpu.make_async_copy(lat.at[c], raw.at[c, g], local_sem.at[1]),
        pltpu.make_async_copy(rot, rot_stage, local_sem.at[2]),
        pltpu.make_async_copy(key_up, key_stage, local_sem.at[3]),
        pltpu.make_async_copy(value_up, value_stage, local_sem.at[4]),
        pltpu.make_async_copy(gain_in, gain, local_sem.at[5]),
    ]
    for load in loads:
        load.start()

    barrier = pltpu.get_barrier_semaphore()

    @pl.loop(1, seqs)
    def _(b):
        pl.semaphore_signal(
            barrier, inc=1, device_id={"ctx": partner(c, b, seqs)}, device_id_type=MESH
        )

    @pl.when(g > 0)
    def _():
        pl.semaphore_signal(barrier, inc=1, device_id={"group": g - 1}, device_id_type=MESH)

    @pl.when(g < planes - 1)
    def _():
        pl.semaphore_signal(barrier, inc=1, device_id={"group": g + 1}, device_id_type=MESH)

    loads[2].wait()

    def pack(s):
        block = rot_stage[s].astype(jnp.float32)
        return jnp.concatenate([block[:half], block[half:]], axis=1).astype(jnp.bfloat16)

    @pl.loop(0, seqs)
    def _(s):
        rot_pack[s] = pack(s)

    rot_raw[c, g] = pack(c)
    loads[0].wait()
    loads[1].wait()
    peers = seqs - 1 + jnp.minimum(g, 1) + jnp.minimum(planes - 1 - g, 1)
    pl.semaphore_wait(barrier, peers)

    def along(p, q, buffer, out_sem, in_sem, to):
        return pltpu.make_async_remote_copy(
            src_ref=buffer.at[q, p], dst_ref=buffer.at[q, p],
            send_sem=out_sem.at[p, q], recv_sem=in_sem.at[p, q],
            device_id={"group": to}, device_id_type=MESH,
        )

    def upward(p, q):
        return along(p, q, raw, up, got, g + 1), along(p, q, rot_raw, up_rot, got_rot, g + 1)

    def downward(p, q):
        return (
            along(p, q, raw, down, got, g - 1),
            along(p, q, rot_raw, down_rot, got_rot, g - 1),
        )

    def across(s, source, buffer, out_sem, in_sem):
        return pltpu.make_async_remote_copy(
            src_ref=source.at[s], dst_ref=buffer.at[c, g],
            send_sem=out_sem.at[s], recv_sem=in_sem.at[g, c],
            device_id={"ctx": s}, device_id_type=MESH,
        )

    def sideways(s):
        return (
            across(s, stage, raw, side, got),
            across(s, rot_pack, rot_raw, side_rot, got_rot),
        )

    def send_up(p, q):
        @pl.when(g < planes - 1)
        def _():
            for copy in upward(p, q):
                copy.start()

    def send_down(p, q):
        @pl.when(g > 0)
        def _():
            for copy in downward(p, q):
                copy.start()

    def arrived(p, q):
        along(p, q, raw, up, got, g).wait_recv()
        along(p, q, rot_raw, up_rot, got_rot, g).wait_recv()

    @pl.loop(1, seqs)
    def _(b):
        across(partner(c, b, seqs), stage, raw, side, got).start()

    send_up(g, c)
    send_down(g, c)

    @pl.loop(1, seqs)
    def _(b):
        across(partner(c, b, seqs), rot_pack, rot_raw, side_rot, got_rot).start()

    loads[3].wait()
    wide[...] = key_stage[...].astype(jnp.float32)
    for h in range(heads):
        key_w[h * key_part : (h + 1) * key_part, :] = (
            wide[pl.ds(h, latent, stride=heads), :].T.astype(jnp.bfloat16)
        )
    loads[4].wait()
    loads[5].wait()
    wide[...] = value_stage[...].astype(jnp.float32)
    size = value_w.shape[1] // heads
    for h in range(heads):
        value_w[:, h * size : (h + 1) * size] = (
            wide[pl.ds(h, latent, stride=heads), :].astype(jnp.bfloat16)
        )

    def expand(q, u):
        first = u * per_unit
        x = raw[q, pl.ds(first, per_unit)].astype(jnp.float32).reshape(UNIT, latent)
        mean = jnp.mean(x * x, axis=-1, keepdims=True)
        rows = (x * lax.rsqrt(mean + 1e-06) * gain[...]).astype(jnp.bfloat16)
        start = pl.multiple_of((q * planes + first) * blk, UNIT)
        wide_keys = lax.dot_general(
            key_w[...], rows, (((1,), (1,)), ((), ())), preferred_element_type=jnp.float32
        ).astype(jnp.bfloat16)
        pieces = []
        for j in range(per_unit):
            both = rot_raw[q, first + j].astype(jnp.float32)
            pieces += [both[:, :rotary], pltpu.roll(both, rotary, 1)[:, :rotary]]
        turned = jnp.concatenate(pieces, axis=0).T.astype(jnp.bfloat16)
        for h in range(heads):
            keys[h, :key_part, pl.ds(start, UNIT)] = wide_keys[h * key_part : (h + 1) * key_part]
            keys[h, key_part:, pl.ds(start, UNIT)] = turned
        wide_values = jnp.dot(rows, value_w[...], preferred_element_type=jnp.float32)
        for h in range(heads):
            mixed[pl.ds(h, UNIT, stride=heads), :] = wide_values[:, h * size : (h + 1) * size]
        at = pl.multiple_of(start * heads, UNIT * heads)
        values[pl.ds(at, UNIT * heads), :] = mixed[...].astype(jnp.bfloat16)

    @pl.loop(1, seqs)
    def _(b):
        q = partner(c, b, seqs)
        arrived(g, q)
        send_up(g, q)
        send_down(g, q)

    @pl.loop(0, planes - 1)
    def _(r):
        @pl.loop(0, seqs)
        def _(b):
            q = partner(c, b, seqs)
            below, above = g - 1 - r, g + 1 + r

            @pl.when(below >= 0)
            def _():
                arrived(below, q)
                send_up(below, q)

            @pl.when(above < planes)
            def _():
                arrived(above, q)
                send_down(above, q)

            @pl.loop(0, planes // per_unit)
            def _(u):
                far = jnp.maximum(g - u * per_unit, (u + 1) * per_unit - 1 - g)

                @pl.when(far == r + 1)
                def _():
                    expand(q, u)

    @pl.loop(1, seqs)
    def _(b):
        for copy in sideways(partner(c, b, seqs)):
            copy.wait_send()

    @pl.loop(0, seqs)
    def _(q):
        @pl.loop(0, planes)
        def _(p):
            @pl.when((p <= g) & (g < planes - 1))
            def _():
                for copy in upward(p, q):
                    copy.wait_send()

            @pl.when((p >= g) & (g > 0))
            def _():
                for copy in downward(p, q):
                    copy.wait_send()


def per_device(latents, rotary_rows, latent_gain, key_up, value_up):
    seqs, planes = lax.axis_size("ctx"), lax.axis_size("group")
    _, blk, latent = latents.shape
    rotary = rotary_rows.shape[2]
    heads, key_part = key_up.shape[1:]
    size = value_up.shape[2]
    length = seqs * planes * blk
    bf16 = jnp.bfloat16
    dma = pltpu.SemaphoreType.DMA
    sent = (planes, seqs)
    in_hbm = functools.partial(pltpu.with_memory_space_constraint, memory_space=pltpu.HBM)
    anywhere = pl.BlockSpec(memory_space=pltpu.HBM)
    inside = pl.BlockSpec(memory_space=pltpu.VMEM)
    keys, values = pl.pallas_call(
        functools.partial(kernel, seqs, planes, heads),
        out_shape=(
            pltpu.VMEM((heads, key_part + rotary, length), bf16),
            pltpu.VMEM((length * heads, size), bf16),
        ),
        in_specs=[anywhere] * 5,
        out_specs=(inside, inside),
        scratch_shapes=[
            pltpu.VMEM((seqs, blk, latent), bf16),
            pltpu.VMEM((seqs, planes, blk, latent), bf16),
            pltpu.VMEM((seqs, blk, rotary), bf16),
            pltpu.VMEM((seqs, blk // 2, 2 * rotary), bf16),
            pltpu.VMEM((seqs, planes, blk // 2, 2 * rotary), bf16),
            pltpu.VMEM((latent * heads, key_part), bf16),
            pltpu.VMEM((latent * heads, size), bf16),
            pltpu.VMEM((latent * heads, size), jnp.float32),
            pltpu.VMEM((heads * key_part, latent), bf16),
            pltpu.VMEM((latent, heads * size), bf16),
            pltpu.VMEM((UNIT * heads, size), jnp.float32),
            pltpu.VMEM((1, latent), jnp.float32),
            dma((6,)),
            dma(sent), dma(sent), dma(sent), dma(sent), dma(sent), dma(sent),
            dma((seqs,)), dma((seqs,)),
        ],
        compiler_params=pltpu.CompilerParams(
            collective_id=0, has_side_effects=True, vmem_limit_bytes=32 * 1024 * 1024
        ),
    )(
        in_hbm(latents),
        in_hbm(rotary_rows),
        in_hbm(latent_gain.reshape(1, latent)),
        in_hbm(key_up.reshape(latent * heads, key_part)),
        in_hbm(value_up.reshape(latent * heads, size)),
    )
    return keys[None], values.reshape(1, length, heads, size)


def solution(mesh):
    in_specs = (
        P("ens", ("ctx", "group"), None),
        P("ens", ("ctx", "group"), None),
        P(),
        P("ens", "group", None),
        P("ens", "group", None),
    )
    out_specs = (P(("ens", "ctx"), "group", None, None), P(("ens", "ctx"), None, "group", None))
    return jax.shard_map(
        per_device, mesh=mesh, in_specs=in_specs, out_specs=out_specs, check_vma=False
    )
```

time: 66.7 us -> 31.5 us (0.47)
  Pallas kernels: 0 us -> 28.6 us
  blocking collectives: 27.5 us -> 0 us
  between operations: 14.1 us -> 0.64 us
  waiting for transfers between devices: 9.92 us -> 0 us
  other arithmetic: 3.68 us -> 0 us
  starting transfers between devices: 3.3 us -> 0 us
  local copies, waits for them, and re-layouts: 5.03 us -> 2.11 us
  matrix products: 2.67 us -> 0 us
    pallas_call x0 -> x1, Pallas kernels: none -> 28.6 us  [per_device(): pl.pallas_call(functools.partial(kernel, seqs, planes, heads), out_shape=...]
    all_gather x1 -> x0, blocking collectives: 16.7 us -> none  [per_device(): lax.all_gather(rotary_cut, 'group', axis=2, tiled=True)]
    all_to_all x1 -> x0, blocking collectives: 10.8 us -> none  [per_device(): lax.all_to_all(rows_ready, 'ctx', split_axis=0, concat_axis=1, tiled=True)]
    all_gather x1 -> x0, waiting for transfers between devices: 5.51 us -> none  [per_device(): lax.all_gather(rows_cut, 'group', axis=2, tiled=True)]
    all_to_all x1 -> x0, waiting for transfers between devices: 4.39 us -> none  [per_device(): lax.all_to_all(rotary_rows, 'ctx', split_axis=0, concat_axis=1, tiled=True)]
    all_to_all x1 -> x0, starting transfers between devices: 3.26 us -> none  [per_device(): lax.all_to_all(rotary_rows, 'ctx', split_axis=0, concat_axis=1, tiled=True)]
    unnamed x10 -> x2, local copies, waits for them, and re-layouts: 4.85 us -> 2.11 us
    unnamed x1 -> x0, matrix products: 1.96 us -> none
  transfers between devices with their start and end apart: 2 -> 0, of which waited for: 2 -> 0; matrix products, arithmetic and copies ran while one was open for 3% -> 0% of each run, Pallas kernels for 0% -> 0%
where the time goes in v1:
time: 31.5 us; the launch traced here: 31.3 us
  Pallas kernels  28.6 us (91%)
  local copies, waits for them, and re-layouts  2.11 us (7%)
  between operations  0.64 us (2%)
    pallas_call x1, Pallas kernels, per_device(): pl.pallas_call(functools.partial(kernel, seqs, planes, heads), out_shape=...  28.6 us
    unnamed x2, local copies, waits for them, and re-layouts  2.11 us

profile of v1, /device:TPU:0, one launch (start us, length us, event | category | flops | bytes accessed | tf_op | source)
XLA Modules:
  0.0 31.3 jit_solution(14661318906913944824)
XLA Ops:
  0.6 28.6 %shard_map.68 = (bf16[4,192,1024]{2,1,0:T(8,128)(2,1)S(1)}, bf16[4096,128]{1,0:T(8,128)(2,1)S(1)}) custom-call(bf16[4,64,512]{2,1,0:T(8,128)(2,1)} %lat.1, bf16[4,64,64]{2,1,0:T(8,128)(2,1)} %rot.1, f32[1,512]{1,0:T(1,128)} %bitcast.9, bf16[2048,128]{1,0:T(8,128)(2,1)} %bitcast.7, bf16[2048,128]{1,0:T(8,128)(2,1)} %bitcast.8), custom_call_target="tpu_custom_call" | custom-call | tf_op jit(solution)/shard_map/pallas_call | solution.py:240
  29.2 1.1 %copy.9 = bf16[1,4,192,1024]{3,2,1,0:T(8,128)(2,1)} copy(bf16[1,4,192,1024]{3,2,1,0:T(8,128)(2,1)S(1)} %bitcast.5) | data formatting | bytes 3145728
  30.3 1.0 %copy.10 = bf16[1,1024,4,128]{3,2,1,0:T(4,128)(2,1)} copy(bf16[1,1024,4,128]{3,2,1,0:T(4,128)(2,1)S(1)} %bitcast.6) | data formatting | bytes 2097152

commit v2 on v1

v2 whole, which is shorter than its diff:
```python
import functools

import jax
import jax.numpy as jnp
from jax import lax
from jax.experimental import pallas as pl
from jax.experimental.pallas import tpu as pltpu
from jax.sharding import PartitionSpec as P

MESH = pl.DeviceIdType.MESH
LANES = 128


def partner(me, step, count):
    if count & (count - 1):
        return lax.rem(me + step, count)
    total, bit = 0, 1
    while bit < count:
        total = total + bit * lax.rem(me // bit + step // bit, 2)
        bit *= 2
    return total


def kernel(
    seqs, planes, heads, rotary,
    lat, rot, gain_in, key_up, value_up, keys, values,
    stage, raw, mid, rot_stage, key_stage, value_stage,
    wide, key_w, value_w, mixed, gain,
    lat_sem, local_sem, got, mid_got, own_up, own_down, side, mid_side, up, down,
):
    c, g = lax.axis_index("ctx"), lax.axis_index("group")
    blk, latent = lat.shape[1:]
    slabs = latent // LANES
    tail = slabs * blk
    half = blk // 2
    per_unit = LANES // blk
    key_part = key_w.shape[0] // heads
    size = value_w.shape[1] // heads

    lat_loads = [
        pltpu.make_async_copy(
            lat.at[:, :, pl.ds(k * LANES, LANES)],
            stage.at[:, pl.ds(k * blk, blk), :],
            lat_sem.at[k],
        )
        for k in range(slabs)
    ]
    loads = [
        pltpu.make_async_copy(rot, rot_stage, local_sem.at[0]),
        pltpu.make_async_copy(key_up, key_stage, local_sem.at[1]),
        pltpu.make_async_copy(value_up, value_stage, local_sem.at[2]),
        pltpu.make_async_copy(gain_in, gain, local_sem.at[3]),
    ]
    loads[0].start()
    for load in lat_loads + loads[1:]:
        load.start()

    barrier = pltpu.get_barrier_semaphore()

    @pl.loop(1, seqs)
    def _(b):
        pl.semaphore_signal(
            barrier, inc=1, device_id={"ctx": partner(c, b, seqs)}, device_id_type=MESH
        )

    @pl.when(g > 0)
    def _():
        pl.semaphore_signal(barrier, inc=1, device_id={"group": g - 1}, device_id_type=MESH)

    @pl.when(g < planes - 1)
    def _():
        pl.semaphore_signal(barrier, inc=1, device_id={"group": g + 1}, device_id_type=MESH)

    loads[0].wait()

    @pl.loop(0, seqs)
    def _(s):
        block = rot_stage[s].astype(jnp.float32)
        both = jnp.concatenate([block[:half], block[half:]], axis=1)
        stage[s, pl.ds(tail, half), :] = both.astype(jnp.bfloat16)

    for load in lat_loads:
        load.wait()
    peers = seqs - 1 + jnp.minimum(g, 1) + jnp.minimum(planes - 1 - g, 1)
    pl.semaphore_wait(barrier, peers)

    def remote(src, dst, out_sem, in_sem, to):
        return pltpu.make_async_remote_copy(
            src_ref=src, dst_ref=dst, send_sem=out_sem, recv_sem=in_sem,
            device_id=to, device_id_type=MESH,
        )

    def own_out(s, way, out_sem, to):
        return remote(
            stage.at[s], mid.at[way, s], out_sem.at[s], mid_got.at[way, s], {"group": to}
        )

    def own_along(out_sem, to):
        return remote(stage.at[c], raw.at[c, g], out_sem.at[c], got.at[g, c], {"group": to})

    def own_side(s):
        return remote(stage.at[s], raw.at[c, g], side.at[s], got.at[g, c], {"ctx": s})

    def scatter(way, s, p):
        return remote(
            mid.at[way, s], raw.at[c, p], mid_side.at[way, s], got.at[p, c], {"ctx": s}
        )

    def relay(p, q, out_sem, to):
        return remote(
            raw.at[q, p], raw.at[q, p], out_sem.at[p, q], got.at[p, q], {"group": to}
        )

    def arrived(p, q):
        relay(p, q, up, g).wait_recv()

    def relay_up(p, q):
        @pl.when(g < planes - 1)
        def _():
            relay(p, q, up, g + 1).start()

    def relay_down(p, q):
        @pl.when(g > 0)
        def _():
            relay(p, q, down, g - 1).start()

    def other(i):
        return partner(c, jnp.where(i == 1, seqs - 1, i - 1), seqs)

    @pl.loop(1, seqs)
    def _(i):
        s = other(i)

        @pl.when(g < planes - 1)
        def _():
            own_out(s, 0, own_up, g + 1).start()

        @pl.when(g > 0)
        def _():
            own_out(s, 1, own_down, g - 1).start()

        @pl.when(i == 1)
        def _():
            @pl.when(g < planes - 1)
            def _():
                own_along(own_up, g + 1).start()

            @pl.when(g > 0)
            def _():
                own_along(own_down, g - 1).start()

    @pl.loop(1, seqs)
    def _(i):
        own_side(partner(c, i, seqs)).start()

    raw[c, g] = stage[c]
    loads[1].wait()
    wide[...] = key_stage[...].astype(jnp.float32)
    for h in range(heads):
        key_w[h * key_part : (h + 1) * key_part, :] = (
            wide[pl.ds(h, latent, stride=heads), :].T.astype(jnp.bfloat16)
        )

    @pl.loop(1, seqs)
    def _(i):
        s = other(i)

        @pl.when(g > 0)
        def _():
            own_out(s, 0, own_up, g).wait_recv()
            scatter(0, s, g - 1).start()

        @pl.when(g < planes - 1)
        def _():
            own_out(s, 1, own_down, g).wait_recv()
            scatter(1, s, g + 1).start()

        @pl.when(i == 1)
        def _():
            @pl.when(g > 0)
            def _():
                arrived(g - 1, c)
                relay_up(g - 1, c)

            @pl.when(g < planes - 1)
            def _():
                arrived(g + 1, c)
                relay_down(g + 1, c)

    loads[2].wait()
    loads[3].wait()
    wide[...] = value_stage[...].astype(jnp.float32)
    for h in range(heads):
        value_w[:, h * size : (h + 1) * size] = (
            wide[pl.ds(h, latent, stride=heads), :].astype(jnp.bfloat16)
        )

    def expand(q, u):
        first = u * per_unit
        x = jnp.concatenate(
            [
                raw[q, pl.ds(first, per_unit), k * blk : (k + 1) * blk, :]
                .astype(jnp.float32)
                .reshape(LANES, LANES)
                for k in range(slabs)
            ],
            axis=1,
        )
        mean = jnp.mean(x * x, axis=-1, keepdims=True)
        rows = (x * lax.rsqrt(mean + 1e-06) * gain[...]).astype(jnp.bfloat16)
        start = pl.multiple_of((q * planes + first) * blk, LANES)
        wide_keys = lax.dot_general(
            key_w[...], rows, (((1,), (1,)), ((), ())), preferred_element_type=jnp.float32
        ).astype(jnp.bfloat16)
        pieces = []
        for j in range(per_unit):
            both = raw[q, first + j, tail:, :].astype(jnp.float32)
            pieces += [both[:, :rotary], pltpu.roll(both, rotary, 1)[:, :rotary]]
        turned = jnp.concatenate(pieces, axis=0).T.astype(jnp.bfloat16)
        for h in range(heads):
            keys[h, :key_part, pl.ds(start, LANES)] = wide_keys[h * key_part : (h + 1) * key_part]
            keys[h, key_part:, pl.ds(start, LANES)] = turned
        wide_values = jnp.dot(rows, value_w[...], preferred_element_type=jnp.float32)
        for h in range(heads):
            mixed[pl.ds(h, LANES, stride=heads), :] = wide_values[:, h * size : (h + 1) * size]
        at = pl.multiple_of(start * heads, LANES * heads)
        values[pl.ds(at, LANES * heads), :] = mixed[...].astype(jnp.bfloat16)

    def settle(r, q):
        @pl.loop(0, planes // per_unit)
        def _(u):
            far = jnp.maximum(g - u * per_unit, (u + 1) * per_unit - 1 - g)

            @pl.when(far == r + 1)
            def _():
                expand(q, u)

    @pl.loop(1, seqs)
    def _(i):
        q = other(i)

        @pl.when(g > 0)
        def _():
            arrived(g - 1, q)
            relay_up(g - 1, q)

        @pl.when(g < planes - 1)
        def _():
            arrived(g + 1, q)
            relay_down(g + 1, q)

    @pl.loop(1, seqs)
    def _(i):
        arrived(g, other(i))

    @pl.loop(0, planes - 1)
    def _(r):
        @pl.loop(0, seqs)
        def _(i):
            q = jnp.where(i == 0, c, other(i))
            below, above = g - 1 - r, g + 1 + r

            @pl.when((r > 0) & (below >= 0))
            def _():
                arrived(below, q)
                relay_up(below, q)

            @pl.when((r > 0) & (above < planes))
            def _():
                arrived(above, q)
                relay_down(above, q)

            settle(r, q)

    @pl.loop(0, seqs)
    def _(s):
        @pl.when(g < planes - 1)
        def _():
            own_out(s, 0, own_up, g).wait_send()

        @pl.when(g > 0)
        def _():
            own_out(s, 1, own_down, g).wait_send()

        @pl.when(s != c)
        def _():
            own_side(s).wait_send()

            @pl.when(g > 0)
            def _():
                scatter(0, s, g).wait_send()

            @pl.when(g < planes - 1)
            def _():
                scatter(1, s, g).wait_send()

        @pl.loop(0, planes)
        def _(p):
            @pl.when((p < g) & (g < planes - 1))
            def _():
                relay(p, s, up, g).wait_send()

            @pl.when((p > g) & (g > 0))
            def _():
                relay(p, s, down, g).wait_send()


def per_device(latents, rotary_rows, latent_gain, key_up, value_up):
    seqs, planes = lax.axis_size("ctx"), lax.axis_size("group")
    _, blk, latent = latents.shape
    rotary = rotary_rows.shape[2]
    heads, key_part = key_up.shape[1:]
    size = value_up.shape[2]
    length = seqs * planes * blk
    packed = (blk * (latent + rotary) // LANES, LANES)
    bf16 = jnp.bfloat16
    dma = pltpu.SemaphoreType.DMA
    in_hbm = functools.partial(pltpu.with_memory_space_constraint, memory_space=pltpu.HBM)
    outer = pl.BlockSpec(memory_space=pltpu.HBM)
    inside = pl.BlockSpec(memory_space=pltpu.VMEM)
    keys, values = pl.pallas_call(
        functools.partial(kernel, seqs, planes, heads, rotary),
        out_shape=(
            pltpu.VMEM((heads, key_part + rotary, length), bf16),
            pltpu.VMEM((length * heads, size), bf16),
        ),
        in_specs=[outer] * 5,
        out_specs=(inside, inside),
        scratch_shapes=[
            pltpu.VMEM((seqs, *packed), bf16),
            pltpu.VMEM((seqs, planes, *packed), bf16),
            pltpu.VMEM((2, seqs, *packed), bf16),
            pltpu.VMEM((seqs, blk, rotary), bf16),
            pltpu.VMEM((latent * heads, key_part), bf16),
            pltpu.VMEM((latent * heads, size), bf16),
            pltpu.VMEM((latent * heads, size), jnp.float32),
            pltpu.VMEM((heads * key_part, latent), bf16),
            pltpu.VMEM((latent, heads * size), bf16),
            pltpu.VMEM((LANES * heads, size), jnp.float32),
            pltpu.VMEM((1, latent), jnp.float32),
            dma((latent // LANES,)),
            dma((4,)),
            dma((planes, seqs)),
            dma((2, seqs)),
            dma((seqs,)), dma((seqs,)), dma((seqs,)),
            dma((2, seqs)),
            dma((planes, seqs)), dma((planes, seqs)),
        ],
        compiler_params=pltpu.CompilerParams(
            collective_id=0, has_side_effects=True, vmem_limit_bytes=32 * 1024 * 1024
        ),
    )(
        in_hbm(latents),
        in_hbm(rotary_rows),
        in_hbm(latent_gain.reshape(1, latent)),
        in_hbm(key_up.reshape(latent * heads, key_part)),
        in_hbm(value_up.reshape(latent * heads, size)),
    )
    return keys[None], values.reshape(1, length, heads, size)


def solution(mesh):
    in_specs = (
        P("ens", ("ctx", "group"), None),
        P("ens", ("ctx", "group"), None),
        P(),
        P("ens", "group", None),
        P("ens", "group", None),
    )
    out_specs = (P(("ens", "ctx"), "group", None, None), P(("ens", "ctx"), None, "group", None))
    return jax.shard_map(
        per_device, mesh=mesh, in_specs=in_specs, out_specs=out_specs, check_vma=False
    )
```

time: 31.5 us -> 30.7 us (0.975)
  Pallas kernels: 28.6 us -> 27.7 us
    pallas_call x1, Pallas kernels: 28.6 us -> 27.7 us  [per_device(): pl.pallas_call(functools.partial(kernel, seqs, planes, heads, rotary), ou...]
where the time goes in v2:
time: 30.7 us; the launch traced here: 30.5 us
  Pallas kernels  27.7 us (90%)
  local copies, waits for them, and re-layouts  2.11 us (7%)
  between operations  0.64 us (2%)
    pallas_call x1, Pallas kernels, per_device(): pl.pallas_call(functools.partial(kernel, seqs, planes, heads, rotary), ou...  27.7 us
    unnamed x2, local copies, waits for them, and re-layouts  2.11 us

profile of v2, /device:TPU:0, one launch (start us, length us, event | category | flops | bytes accessed | tf_op | source)
XLA Modules:
  0.0 30.5 jit_solution(11095084286350512914)
XLA Ops:
  0.6 27.7 %shard_map.68 = (bf16[4,192,1024]{2,1,0:T(8,128)(2,1)S(1)}, bf16[4096,128]{1,0:T(8,128)(2,1)S(1)}) custom-call(bf16[4,64,512]{2,1,0:T(8,128)(2,1)} %lat.1, bf16[4,64,64]{2,1,0:T(8,128)(2,1)} %rot.1, f32[1,512]{1,0:T(1,128)} %bitcast.9, bf16[2048,128]{1,0:T(8,128)(2,1)} %bitcast.7, bf16[2048,128]{1,0:T(8,128)(2,1)} %bitcast.8), custom_call_target="tpu_custom_call" | custom-call | tf_op jit(solution)/shard_map/pallas_call | solution.py:321
  28.4 1.1 %copy.9 = bf16[1,4,192,1024]{3,2,1,0:T(8,128)(2,1)} copy(bf16[1,4,192,1024]{3,2,1,0:T(8,128)(2,1)S(1)} %bitcast.5) | data formatting | bytes 3145728
  29.5 1.0 %copy.10 = bf16[1,1024,4,128]{3,2,1,0:T(4,128)(2,1)} copy(bf16[1,1024,4,128]{3,2,1,0:T(4,128)(2,1)S(1)} %bitcast.6) | data formatting | bytes 2097152

commit v3 on v2

--- a/solution.py
+++ b/solution.py
@@ -161,32 +161,6 @@
             wide[pl.ds(h, latent, stride=heads), :].T.astype(jnp.bfloat16)
         )
 
-    @pl.loop(1, seqs)
-    def _(i):
-        s = other(i)
-
-        @pl.when(g > 0)
-        def _():
-            own_out(s, 0, own_up, g).wait_recv()
-            scatter(0, s, g - 1).start()
-
-        @pl.when(g < planes - 1)
-        def _():
-            own_out(s, 1, own_down, g).wait_recv()
-            scatter(1, s, g + 1).start()
-
-        @pl.when(i == 1)
-        def _():
-            @pl.when(g > 0)
-            def _():
-                arrived(g - 1, c)
-                relay_up(g - 1, c)
-
-            @pl.when(g < planes - 1)
-            def _():
-                arrived(g + 1, c)
-                relay_down(g + 1, c)
-
     loads[2].wait()
     loads[3].wait()
     wide[...] = value_stage[...].astype(jnp.float32)
@@ -194,6 +168,32 @@
         value_w[:, h * size : (h + 1) * size] = (
             wide[pl.ds(h, latent, stride=heads), :].astype(jnp.bfloat16)
         )
+
+    @pl.loop(1, seqs)
+    def _(i):
+        s = other(i)
+
+        @pl.when(g > 0)
+        def _():
+            own_out(s, 0, own_up, g).wait_recv()
+            scatter(0, s, g - 1).start()
+
+        @pl.when(g < planes - 1)
+        def _():
+            own_out(s, 1, own_down, g).wait_recv()
+            scatter(1, s, g + 1).start()
+
+        @pl.when(i == 1)
+        def _():
+            @pl.when(g > 0)
+            def _():
+                arrived(g - 1, c)
+                relay_up(g - 1, c)
+
+            @pl.when(g < planes - 1)
+            def _():
+                arrived(g + 1, c)
+                relay_down(g + 1, c)
 
     def expand(q, u):
         first = u * per_unit
@@ -226,12 +226,13 @@
         at = pl.multiple_of(start * heads, LANES * heads)
         values[pl.ds(at, LANES * heads), :] = mixed[...].astype(jnp.bfloat16)
 
-    def settle(r, q):
+    def settle(q, low, high):
         @pl.loop(0, planes // per_unit)
         def _(u):
             far = jnp.maximum(g - u * per_unit, (u + 1) * per_unit - 1 - g)
-
-            @pl.when(far == r + 1)
+            far = jnp.maximum(far, 1)
+
+            @pl.when((far >= low) & (far <= high))
             def _():
                 expand(q, u)
 
@@ -253,24 +254,24 @@
     def _(i):
         arrived(g, other(i))
 
-    @pl.loop(0, planes - 1)
+    @pl.loop(1, max(planes - 1, 2))
     def _(r):
         @pl.loop(0, seqs)
         def _(i):
             q = jnp.where(i == 0, c, other(i))
             below, above = g - 1 - r, g + 1 + r
 
-            @pl.when((r > 0) & (below >= 0))
+            @pl.when(below >= 0)
             def _():
                 arrived(below, q)
                 relay_up(below, q)
 
-            @pl.when((r > 0) & (above < planes))
+            @pl.when(above < planes)
             def _():
                 arrived(above, q)
                 relay_down(above, q)
 
-            settle(r, q)
+            settle(q, r, jnp.where(r == planes - 2, r + 1, r))
 
     @pl.loop(0, seqs)
     def _(s):
@@ -303,6 +304,24 @@
             @pl.when((p > g) & (g > 0))
             def _():
                 relay(p, s, down, g).wait_send()
+
+
+def store(keys, values, keys_out, values_out, sems):
+    pieces = sems.shape[0] // 2
+    rows = values.shape[0] // pieces
+    heads = keys.shape[0] // pieces
+    copies = []
+    for i in range(pieces):
+        part = pl.ds(i * heads, heads)
+        copies.append(pltpu.make_async_copy(keys.at[part], keys_out.at[part], sems.at[2 * i]))
+        part = pl.ds(i * rows, rows)
+        copies.append(
+            pltpu.make_async_copy(values.at[part], values_out.at[part], sems.at[2 * i + 1])
+        )
+    for copy in copies:
+        copy.start()
+    for copy in copies:
+        copy.wait()
 
 
 def per_device(latents, rotary_rows, latent_gain, key_up, value_up):
@@ -356,6 +375,17 @@
         in_hbm(key_up.reshape(latent * heads, key_part)),
         in_hbm(value_up.reshape(latent * heads, size)),
     )
+    keys, values = pl.pallas_call(
+        store,
+        out_shape=(
+            jax.ShapeDtypeStruct(keys.shape, bf16),
+            jax.ShapeDtypeStruct(values.shape, bf16),
+        ),
+        in_specs=[inside, inside],
+        out_specs=(outer, outer),
+        scratch_shapes=[dma((2 * heads,))],
+        compiler_params=pltpu.CompilerParams(vmem_limit_bytes=16 * 1024 * 1024),
+    )(keys, values)
     return keys[None], values.reshape(1, length, heads, size)
 
 

time: 30.7 us -> 30 us (0.977)
  local copies, waits for them, and re-layouts: 2.11 us -> 0 us
  Pallas kernels: 27.7 us -> 29.3 us
    unnamed x2 -> x0, local copies, waits for them, and re-layouts: 2.11 us -> none
    pallas_call x0 -> x1, Pallas kernels: none -> 1.55 us  [per_device(): pl.pallas_call(store, out_shape=(jax.ShapeDtypeStruct(keys.shape, bf16),...]
where the time goes in v3:
time: 30 us; the launch traced here: 29.9 us
  Pallas kernels  29.3 us (98%)
  between operations  0.64 us (2%)
    pallas_call x1, Pallas kernels, per_device(): pl.pallas_call(functools.partial(kernel, seqs, planes, heads, rotary), ou...  27.7 us
    pallas_call x1, Pallas kernels, per_device(): pl.pallas_call(store, out_shape=(jax.ShapeDtypeStruct(keys.shape, bf16),...  1.55 us

profile of v3, /device:TPU:0, one launch (start us, length us, event | category | flops | bytes accessed | tf_op | source)
XLA Modules:
  0.0 29.9 jit_solution(7009974054770588706)
XLA Ops:
  0.6 27.7 %shard_map.68 = (bf16[4,192,1024]{2,1,0:T(8,128)(2,1)S(1)}, bf16[4096,128]{1,0:T(8,128)(2,1)S(1)}) custom-call(bf16[4,64,512]{2,1,0:T(8,128)(2,1)} %lat.1, bf16[4,64,64]{2,1,0:T(8,128)(2,1)} %rot.1, f32[1,512]{1,0:T(1,128)} %bitcast.7, bf16[2048,128]{1,0:T(8,128)(2,1)} %bitcast.5, bf16[2048,128]{1,0:T(8,128)(2,1)} %bitcast.6), custom_call_target="tpu_custom_call" | custom-call | tf_op jit(solution)/shard_map/pallas_call | solution.py:340
  28.3 1.5 %shard_map.69 = (bf16[4,192,1024]{2,1,0:T(8,128)(2,1)}, bf16[4096,128]{1,0:T(8,128)(2,1)}) custom-call(bf16[4,192,1024]{2,1,0:T(8,128)(2,1)S(1)} %get-tuple-element.6.keys, bf16[4096,128]{1,0:T(8,128)(2,1)S(1)} %get-tuple-element.7.values), custom_call_target="tpu_custom_call" | custom-call | tf_op jit(solution)/shard_map/pallas_call | solution.py:378

commit v4 on v3

--- a/solution.py
+++ b/solution.py
@@ -169,31 +169,46 @@
             wide[pl.ds(h, latent, stride=heads), :].astype(jnp.bfloat16)
         )
 
+    low = 2 * g < planes
+
+    def near_first(from_below, from_above):
+        pl.when(low)(from_above)
+        from_below()
+        pl.when(jnp.logical_not(low))(from_above)
+
     @pl.loop(1, seqs)
     def _(i):
         s = other(i)
 
-        @pl.when(g > 0)
-        def _():
-            own_out(s, 0, own_up, g).wait_recv()
-            scatter(0, s, g - 1).start()
-
-        @pl.when(g < planes - 1)
-        def _():
-            own_out(s, 1, own_down, g).wait_recv()
-            scatter(1, s, g + 1).start()
-
-        @pl.when(i == 1)
-        def _():
+        def spread_below():
+            @pl.when(g > 0)
+            def _():
+                own_out(s, 0, own_up, g).wait_recv()
+                scatter(0, s, g - 1).start()
+
+        def spread_above():
+            @pl.when(g < planes - 1)
+            def _():
+                own_out(s, 1, own_down, g).wait_recv()
+                scatter(1, s, g + 1).start()
+
+        near_first(spread_below, spread_above)
+
+        def own_below():
             @pl.when(g > 0)
             def _():
                 arrived(g - 1, c)
                 relay_up(g - 1, c)
 
+        def own_above():
             @pl.when(g < planes - 1)
             def _():
                 arrived(g + 1, c)
                 relay_down(g + 1, c)
+
+        @pl.when(i == 1)
+        def _():
+            near_first(own_below, own_above)
 
     def expand(q, u):
         first = u * per_unit
@@ -240,15 +255,19 @@
     def _(i):
         q = other(i)
 
-        @pl.when(g > 0)
-        def _():
-            arrived(g - 1, q)
-            relay_up(g - 1, q)
-
-        @pl.when(g < planes - 1)
-        def _():
-            arrived(g + 1, q)
-            relay_down(g + 1, q)
+        def next_below():
+            @pl.when(g > 0)
+            def _():
+                arrived(g - 1, q)
+                relay_up(g - 1, q)
+
+        def next_above():
+            @pl.when(g < planes - 1)
+            def _():
+                arrived(g + 1, q)
+                relay_down(g + 1, q)
+
+        near_first(next_below, next_above)
 
     @pl.loop(1, seqs)
     def _(i):

time: 30 us -> 29.6 us (0.987)
  Pallas kernels: 29.3 us -> 28.8 us
    pallas_call x1, Pallas kernels: 27.7 us -> 27.3 us  [per_device(): pl.pallas_call(functools.partial(kernel, seqs, planes, heads, rotary), ou...]
where the time goes in v4:
time: 29.6 us; the launch traced here: 29.4 us
  Pallas kernels  28.8 us (97%)
  between operations  0.64 us (2%)
    pallas_call x1, Pallas kernels, per_device(): pl.pallas_call(functools.partial(kernel, seqs, planes, heads, rotary), ou...  27.3 us
    pallas_call x1, Pallas kernels, per_device(): pl.pallas_call(store, out_shape=(jax.ShapeDtypeStruct(keys.shape, bf16),...  1.55 us

profile of v4, /device:TPU:0, one launch (start us, length us, event | category | flops | bytes accessed | tf_op | source)
XLA Modules:
  0.0 29.4 jit_solution(12788584473197460981)
XLA Ops:
  0.6 27.3 %shard_map.68 = (bf16[4,192,1024]{2,1,0:T(8,128)(2,1)S(1)}, bf16[4096,128]{1,0:T(8,128)(2,1)S(1)}) custom-call(bf16[4,64,512]{2,1,0:T(8,128)(2,1)} %lat.1, bf16[4,64,64]{2,1,0:T(8,128)(2,1)} %rot.1, f32[1,512]{1,0:T(1,128)} %bitcast.7, bf16[2048,128]{1,0:T(8,128)(2,1)} %bitcast.5, bf16[2048,128]{1,0:T(8,128)(2,1)} %bitcast.6), custom_call_target="tpu_custom_call" | custom-call | tf_op jit(solution)/shard_map/pallas_call | solution.py:359
  27.9 1.5 %shard_map.69 = (bf16[4,192,1024]{2,1,0:T(8,128)(2,1)}, bf16[4096,128]{1,0:T(8,128)(2,1)}) custom-call(bf16[4,192,1024]{2,1,0:T(8,128)(2,1)S(1)} %get-tuple-element.6.keys, bf16[4096,128]{1,0:T(8,128)(2,1)S(1)} %get-tuple-element.7.values), custom_call_target="tpu_custom_call" | custom-call | tf_op jit(solution)/shard_map/pallas_call | solution.py:397
